TPU v7x, 32 devices: a whole 2x2x4 slice. The times are simulated.
32 devices in a mesh: section: 1, grp: 16 (over z, x, core), tp: 2 (over y).
Axes of the slice: x: 2, y: 2, z: 4, core: 2. Of those that a mesh axis runs over, the one named last changes fastest.
Arguments:
- partials: bfloat16 [2, 1, 2048, 8192], P('tp', 'section', 'grp'), may hold values from -3 to 3
- residual: bfloat16 [1, 2048, 8192], P('section', 'grp', 'tp'), may hold values from -300 to 300
- norm_gain: bfloat16 [8192], replicated, may hold values from 0.099609375 to 1.8984375
- w_query: bfloat16 [8192, 8192], P('grp', ('section', 'tp')), may hold values from -0.0625 to 0.0625
- w_keyval: bfloat16 [8192, 2048], P('grp', ('section', 'tp')), may hold values from -0.0625 to 0.0625
- bias_query: bfloat16 [8192], P(('section', 'tp')), may hold values from -3 to 3
- bias_keyval: bfloat16 [2048], P(('section', 'tp')), may hold values from -3 to 3
Outputs:
- hidden: bfloat16 [1, 2048, 8192], P('section', 'grp', 'tp')
- query: bfloat16 [1, 2048, 8192], P(None, 'grp', ('section', 'tp'))
- keyval: bfloat16 [1, 2048, 2048], P(None, 'grp', ('section', 'tp'))
All inputs are finite; a program needn't handle non-finite values.
Results may differ from a plain program's by a relative error of at most 0.01.
Values may be sent and summed in bfloat16 or wider, within the bound.
A program may use at most 192 MiB of HBM per device.

v0:
```python
import jax
import jax.numpy as jnp
from jax import lax
from jax.sharding import PartitionSpec as P

epsilon = 1e-06


def spread_tp(normed):
    return lax.all_gather(normed, "tp", axis=2, tiled=True)


def local(partials, residual, norm_gain, w_query, w_keyval, bias_query, bias_keyval):
    model_width = norm_gain.shape[0]
    partial_term = partials[0].astype(jnp.float32)
    scaled_gain = norm_gain.astype(jnp.float32)
    summed = lax.psum_scatter(
        partial_term.astype(jnp.bfloat16), "tp", scatter_dimension=2, tiled=True
    ).astype(jnp.float32)
    hidden = (residual.astype(jnp.float32) + summed).astype(jnp.bfloat16)
    widened = hidden.astype(jnp.float32)
    squares = lax.psum(jnp.sum(widened * widened, axis=-1), "tp")
    feature_share = widened.shape[2]
    offset = lax.axis_index("tp") * feature_share
    local_gain = lax.dynamic_slice_in_dim(scaled_gain, offset, feature_share, 0)
    mean_square = squares[..., None] / model_width
    normed = (widened * lax.rsqrt(mean_square + epsilon) * local_gain).astype(jnp.bfloat16)
    gathered = lax.all_gather(spread_tp(normed), "section", axis=0, tiled=True)
    flattened = gathered.reshape(-1, model_width)
    query_total = jnp.dot(
        flattened,
        lax.all_gather(w_query, "grp", axis=0, tiled=True),
        preferred_element_type=jnp.float32,
    )
    keyval_total = jnp.dot(
        flattened,
        lax.all_gather(w_keyval, "grp", axis=0, tiled=True),
        preferred_element_type=jnp.float32,
    )
    query = (query_total + bias_query.astype(jnp.float32)).astype(jnp.bfloat16)
    keyval = (keyval_total + bias_keyval.astype(jnp.float32)).astype(jnp.bfloat16)
    query = query.reshape(gathered.shape[0], gathered.shape[1], -1)
    keyval = keyval.reshape(gathered.shape[0], gathered.shape[1], -1)
    return (hidden, query, keyval)


def solution(mesh):
    placed = (
        P("tp", "section", "grp", None),
        P("section", "grp", "tp"),
        P(),
        P("grp", ("section", "tp")),
        P("grp", ("section", "tp")),
        P(("section", "tp")),
        P(("section", "tp")),
    )
    return jax.shard_map(
        local,
        mesh=mesh,
        in_specs=placed,
        out_specs=(
            P("section", "grp", "tp"),
            P(None, "grp", ("section", "tp")),
            P(None, "grp", ("section", "tp")),
        ),
        check_vma=False,
    )
```

profile of v0, /device:TPU:26, one launch (start us, length us, event | category | flops | bytes accessed | tf_op | source)
XLA Modules:
  0.0 568.2 jit_solution(15152440889435875697)
XLA Ops:
  7.2 0.0 reduce-scatter.2.cloned.1.call-start
  7.2 0.7 reduce-scatter.2.cloned.1.call-update
  7.9 0.0 all-gather.4.cloned.1.call-start
  8.0 35.1 %reduce-scatter.2.cloned.1.call-done = bf16[1,128,4096]{2,1,0:T(8,128)(2,1)} async-done(((bf16[1,128,8192]{2,1,0:T(8,128)(2,1)}), bf16[1,128,4096]{2,1,0:T(8,128)(2,1)}) %reduce-scatter.2.cloned.1.call-update) | async-done | bytes 1048592 | tf_op jit(solution)/shard_map/reduce_scatter | solution.py:17
  43.1 0.0 copy-done.2
  43.1 1.7 fusion.2
  44.8 0.0 copy-start.1
  44.8 4.9 psum.7
  49.8 1.3 fusion.4
  51.1 0.0 all-gather.4.cloned.1.call-update
  51.1 0.0 all-gather.8.cloned.1.call-start
  51.1 0.7 all-gather.8.cloned.1.call-update
  51.8 0.0 copy-start.3
  51.9 0.0 copy-start.5
  51.9 0.0 all-gather.6.cloned.1.call-start
  51.9 0.5 all-gather.6.cloned.1.call-update
  52.4 0.1 copy-done.3
  52.5 0.0 copy-done.5
  52.6 31.8 %all-gather.4.cloned.1.call-done = bf16[1,128,8192]{2,1,0:T(8,128)(2,1)} async-done(((bf16[1,128,4096]{2,1,0:T(8,128)(2,1)}), bf16[1,128,8192]{2,1,0:T(8,128)(2,1)}) %all-gather.4.cloned.1.call-update) | async-done | bytes 2097168 | tf_op jit(solution)/shard_map/all_gather | solution.py:10
  84.3 125.8 %all-gather.8.cloned.1.call-done = bf16[8192,1024]{1,0:T(8,128)(2,1)} async-done(((bf16[512,1024]{1,0:T(8,128)(2,1)}), bf16[8192,1024]{1,0:T(8,128)(2,1)}) %all-gather.8.cloned.1.call-update) | async-done | bytes 16777232 | tf_op jit(solution)/shard_map/all_gather | solution.py:37
  210.1 9.4 %fusion.14 = bf16[1,128,1024]{2,1,0:T(8,128)(2,1)} fusion(bf16[8192,1024]{1,0:T(8,128)(2,1)} %all-gather.8.cloned.1.call-done, bf16[1,128,8192]{2,1,0:T(8,128)(2,1)} %all-gather.4.cloned.1.call-done, f32[1024]{0:T(1024)S(1)} %convert_element_type.40), kind=kOutput, calls=%fused_computation.14 | convolution fusion | flops 2147745792 | bytes 19140608 | tf_op jit(solution)/shard_map/dot_general | solution.py:35
  219.5 318.2 %all-gather.6.cloned.1.call-done = bf16[8192,4096]{1,0:T(8,128)(2,1)} async-done(((bf16[512,4096]{1,0:T(8,128)(2,1)}), bf16[8192,4096]{1,0:T(8,128)(2,1)}) %all-gather.6.cloned.1.call-update) | async-done | bytes 67108880 | tf_op jit(solution)/shard_map/all_gather | solution.py:32
  537.8 0.0 copy-done
  537.8 23.9 %fusion.1 = bf16[1,128,4096]{2,1,0:T(8,128)(2,1)} fusion(bf16[8192,4096]{1,0:T(8,128)(2,1)} %all-gather.6.cloned.1.call-done, bf16[1,128,8192]{2,1,0:T(8,128)(2,1)S(1)} %copy-done, f32[4096]{0:T(1024)S(1)} %convert_element_type.38), kind=kOutput, calls=%fused_computation.2 | convolution fusion | flops 8590983168 | bytes 70270976 | tf_op jit(solution)/shard_map/dot_general | solution.py:30
  (9 shorter events, 0.0 us)
Async XLA Ops:
  7.2 0.8 copy-start.4
  7.2 36.0 %copy-start.2 = (bf16[1,128,4096]{2,1,0:T(8,128)(2,1)S(1)}, bf16[1,128,4096]{2,1,0:T(8,128)(2,1)}, u32[]{:S(2)}) copy-start(bf16[1,128,4096]{2,1,0:T(8,128)(2,1)} %param.8) | copy-start | bytes 3145732
  7.2 35.9 %reduce-scatter.2.cloned.1.call-start = ((), (), s32[]{:S(2)}) async-start(), calls=%async_computation.1 | async-start | bytes 3145728 | tf_op jit(solution)/shard_map/reduce_scatter | solution.py:17
  7.9 76.4 %all-gather.4.cloned.1.call-start = ((), (), s32[]{:S(2)}) async-start(), calls=%async_computation.2 | async-start | bytes 3145728 | tf_op jit(solution)/shard_map/all_gather | solution.py:10
  44.8 7.0 %copy-start.1 = (bf16[1,128,4096]{2,1,0:T(8,128)(2,1)}, bf16[1,128,4096]{2,1,0:T(8,128)(2,1)S(1)}, u32[]{:S(2)}) copy-start(bf16[1,128,4096]{2,1,0:T(8,128)(2,1)S(1)} %get-tuple-element.4) | copy-start | bytes 3145732
  51.1 159.0 %all-gather.8.cloned.1.call-start = ((), (), s32[]{:S(2)}) async-start(), calls=%async_computation.4 | async-start | bytes 17825792 | tf_op jit(solution)/shard_map/all_gather | solution.py:37
  51.8 0.7 copy-start.3
  51.9 0.7 copy-start.5
  51.9 485.9 %all-gather.6.cloned.1.call-start = ((), (), s32[]{:S(2)}) async-start(), calls=%async_computation.3 | async-start | bytes 71303168 | tf_op jit(solution)/shard_map/all_gather | solution.py:32
  84.3 453.4 %copy-start = (bf16[1,128,8192]{2,1,0:T(8,128)(2,1)S(1)}, bf16[1,128,8192]{2,1,0:T(8,128)(2,1)}, u32[]{:S(2)}) copy-start(bf16[1,128,8192]{2,1,0:T(8,128)(2,1)} %all-gather.4.cloned.1.call-done) | copy-start | bytes 6291460
Sparse Core Ops, SparseCore 0:
  10.2 32.8 reduce-scatter.1
  51.2 33.0 all-gather.3
  86.5 123.5 all-gather.7
  211.6 326.1 all-gather.5
where the time goes:
time: 571 us; the launch traced here: 568 us
  waiting for transfers between devices  513 us (90%)
  matrix products  33.3 us (6%)
  between operations  13.8 us (2%)
    all_gather x1, waiting for transfers between devices, local(): lax.all_gather(w_query, 'grp', axis=0, tiled=True)  318 us
    all_gather x1, waiting for transfers between devices, local(): lax.all_gather(w_keyval, 'grp', axis=0, tiled=True)  126 us
    reduce_scatter x1, waiting for transfers between devices, local(): lax.psum_scatter(partial_term.astype(jnp.bfloat16), 'tp', scatter_dimensi...  35.1 us
    all_gather x1, waiting for transfers between devices, spread_tp(): return lax.all_gather(normed, 'tp', axis=2, tiled=True)  31.8 us
    dot_general x1, matrix products, local(): jnp.dot(flattened, lax.all_gather(w_query, 'grp', axis=0, tiled=True), pr...  23.9 us
  transfers between devices with their start and end apart: 4, of which 4 were waited for; matrix products, arithmetic and copies ran while one was open for 2% of the time, Pallas kernels for 0%

commit v1 on v0

v1 whole, which is shorter than its diff:
```python
import jax
import jax.numpy as jnp
from jax import lax
from jax.sharding import PartitionSpec as P

epsilon = 1e-06


def local(partials, residual, norm_gain, w_query, w_keyval, bias_query, bias_keyval):
    model_width = norm_gain.shape[0]
    summed = lax.psum_scatter(
        partials[0], "tp", scatter_dimension=2, tiled=True
    ).astype(jnp.float32)
    hidden = (residual.astype(jnp.float32) + summed).astype(jnp.bfloat16)
    widened = hidden.astype(jnp.float32)
    squares = lax.psum(jnp.sum(widened * widened, axis=-1), "tp")
    feature_share = widened.shape[2]
    offset = lax.axis_index("tp") * feature_share
    local_gain = lax.dynamic_slice_in_dim(norm_gain, offset, feature_share, 0).astype(jnp.float32)
    scaled = (widened * local_gain).astype(jnp.bfloat16)
    scaled = lax.all_gather(scaled, "tp", axis=2, tiled=True)
    gathered_squares = lax.all_gather(squares, "section", axis=0, tiled=True)
    scale = lax.rsqrt(gathered_squares / model_width + epsilon)[..., None]
    exchanged = lax.all_to_all(scaled, "grp", split_axis=2, concat_axis=1, tiled=True)
    exchanged = lax.all_gather(exchanged, "section", axis=0, tiled=True)
    seqs, length, depth = exchanged.shape
    flat = exchanged.reshape(seqs * length, depth)

    def project(weight, bias):
        total = jnp.dot(flat, weight, preferred_element_type=jnp.float32).astype(jnp.bfloat16)
        total = total.reshape(seqs, length, -1)
        own = lax.psum_scatter(total, "grp", scatter_dimension=1, tiled=True)
        return (own.astype(jnp.float32) * scale + bias.astype(jnp.float32)).astype(jnp.bfloat16)

    keyval = project(w_keyval, bias_keyval)
    query = project(w_query, bias_query)
    return (hidden, query, keyval)


def solution(mesh):
    placed = (
        P("tp", "section", "grp", None),
        P("section", "grp", "tp"),
        P(),
        P("grp", ("section", "tp")),
        P("grp", ("section", "tp")),
        P(("section", "tp")),
        P(("section", "tp")),
    )
    return jax.shard_map(
        local,
        mesh=mesh,
        in_specs=placed,
        out_specs=(
            P("section", "grp", "tp"),
            P(None, "grp", ("section", "tp")),
            P(None, "grp", ("section", "tp")),
        ),
        check_vma=False,
    )
```

time: 571 us -> 472 us (0.83)
  waiting for transfers between devices: 513 us -> 298 us
  blocking collectives: 4.93 us -> 57.2 us
  other arithmetic: 3.01 us -> 52.4 us
  local copies, waits for them, and re-layouts: 0.13 us -> 26.9 us
  matrix products: 33.3 us -> 19.7 us
    all_gather x3 -> x1, waiting for transfers between devices: 476 us -> 33.2 us  [local(): scaled = lax.all_gather(scaled, 'tp', axis=2, tiled=True)]
    reduce_scatter x1 -> x3, waiting for transfers between devices: 35.1 us -> 264 us  [the longest x2 229 us: project(): own = lax.psum_scatter(total, 'grp', scatter_dimension=1, tiled=True)]
    all_to_all x0 -> x1, blocking collectives: none -> 52.3 us  [local(): lax.all_to_all(scaled, 'grp', split_axis=2, concat_axis=1, tiled=True)]
    unnamed x0 -> x1, other arithmetic: none -> 45.2 us
    unnamed x12 -> x18, local copies, waits for them, and re-layouts: 0.13 us -> 14.8 us
    dot_general x2, matrix products: 33.3 us -> 19.7 us  [project(): jnp.dot(flat, weight, preferred_element_type=jnp.float32)]
    all_gather x0 -> x1, local copies, waits for them, and re-layouts: none -> 9.49 us  [local(): scaled = lax.all_gather(scaled, 'tp', axis=2, tiled=True)]
  transfers between devices with their start and end apart: 4 -> 4, of which waited for: 4 -> 4; matrix products, arithmetic and copies ran while one was open for 2% -> 3% of each run, Pallas kernels for 0% -> 0%
where the time goes in v1:
time: 472 us; the launch traced here: 468 us
  waiting for transfers between devices  298 us (63%)
  blocking collectives  57.2 us (12%)
  other arithmetic  52.4 us (11%)
  local copies, waits for them, and re-layouts  26.9 us (6%)
  matrix products  19.7 us (4%)
  between operations  13.8 us (3%)
    reduce_scatter x2, waiting for transfers between devices, project(): own = lax.psum_scatter(total, 'grp', scatter_dimension=1, tiled=True)  229 us
    all_to_all x1, blocking collectives, local(): lax.all_to_all(scaled, 'grp', split_axis=2, concat_axis=1, tiled=True)  52.3 us
    unnamed x1, other arithmetic  45.2 us
    reduce_scatter x1, waiting for transfers between devices, local(): lax.psum_scatter(partials[0], 'tp', scatter_dimension=2, tiled=True)  35.1 us
    all_gather x1, waiting for transfers between devices, local(): scaled = lax.all_gather(scaled, 'tp', axis=2, tiled=True)  33.2 us
    dot_general x2, matrix products, project(): jnp.dot(flat, weight, preferred_element_type=jnp.float32)  19.7 us
    unnamed x18, local copies, waits for them, and re-layouts  14.8 us
    all_gather x1, local copies, waits for them, and re-layouts, local(): scaled = lax.all_gather(scaled, 'tp', axis=2, tiled=True)  9.49 us
  transfers between devices with their start and end apart: 4, of which 4 were waited for; matrix products, arithmetic and copies ran while one was open for 3% of the time, Pallas kernels for 0%

profile of v1, /device:TPU:26, one launch (start us, length us, event | category | flops | bytes accessed | tf_op | source)
XLA Modules:
  0.0 468.0 jit_solution(13430152191114884679)
XLA Ops:
  7.2 0.7 reduce-scatter.4.cloned.1.call-update
  8.0 35.1 %reduce-scatter.4.cloned.1.call-done = bf16[1,128,4096]{2,1,0:T(8,128)(2,1)} async-done(((bf16[1,128,8192]{2,1,0:T(8,128)(2,1)}), bf16[1,128,4096]{2,1,0:T(8,128)(2,1)}) %reduce-scatter.4.cloned.1.call-update) | async-done | bytes 1048592 | tf_op jit(solution)/shard_map/reduce_scatter | solution.py:11
  43.1 1.7 fusion.1
  44.8 1.0 copy-done.1
  45.8 1.2 fusion
  47.1 33.2 %all-gather.2.cloned.1.call-done = bf16[1,128,8192]{2,1,0:T(8,128)(2,1)} async-done(((bf16[1,128,4096]{2,1,0:T(8,128)(2,1)}), bf16[1,128,8192]{2,1,0:T(8,128)(2,1)}) %all-gather.2.cloned.1.call-update) | async-done | bytes 2097168 | tf_op jit(solution)/shard_map/all_gather | solution.py:21
  80.3 9.5 %copy.18 = bf16[1,128,8192]{1,0,2:T(2,128)(2,1)} copy(bf16[1,128,8192]{2,1,0:T(8,128)(2,1)} %all-gather.2.cloned.1.call-done) | data formatting | bytes 4194304 | tf_op jit(solution)/shard_map/all_gather | solution.py:21
  89.7 0.5 broadcast.9
  90.3 45.2 %reduce.1 = bf16[8192,128]{1,0:T(8,128)(2,1)S(1)} reduce(bf16[8192,1,128]{2,1,0:T(2,128)(2,1)} %bitcast.18, bf16[]{:T(256)} %broadcast.9), dimensions={1}, to_apply=%bitcast.12.reduce_sub_computation | reduce | bytes 4194306
  135.4 2.1 reshape.33
  137.5 52.3 %all_to_all.15 = bf16[16,2,32768]{2,1,0:T(2,128)(2,1)S(1)} all-to-all(bf16[16,2,32768]{2,1,0:T(2,128)(2,1)} %reshape.33), channel_id=1, replica_groups=mesh['section'=1,'grp'=16,'tp'=2] {'grp'}, dimensions={0} | all-to-all | bytes 4194304 | tf_op jit(solution)/shard_map/all_to_all | solution.py:24
  189.8 6.8 %reshape.34 = bf16[8192,1,128]{2,1,0:T(2,128)(2,1)} reshape(bf16[16,2,32768]{2,1,0:T(2,128)(2,1)S(1)} %all_to_all.15) | data formatting | bytes 4194304
  196.6 2.5 copy.20
  199.0 2.6 copy.19
  201.6 5.9 %convert_bitcast_fusion.1 = bf16[1,2048,1024]{2,1,0:T(8,128)(2,1)} fusion(bf16[2048,512]{1,0:T(8,128)(2,1)} %bitcast.22, bf16[512,1024]{1,0:T(8,128)(2,1)S(1)} %copy-done), kind=kOutput, calls=%fused_computation.1 | convolution fusion | flops 2149580800 | bytes 7340032 | tf_op jit(solution)/shard_map/dot_general | solution.py:30
  207.5 0.2 reduce-scatter.6.cloned.1.call-start
  207.8 1.3 copy-done.2
  209.1 13.8 %convert_bitcast_fusion = bf16[1,2048,4096]{2,1,0:T(8,128)(2,1)} fusion(bf16[2048,512]{1,0:T(8,128)(2,1)S(1)} %bitcast.23, bf16[512,4096]{1,0:T(8,128)(2,1)} %param.10), kind=kOutput, calls=%fused_computation | convolution fusion | flops 8598323200 | bytes 23068672 | tf_op jit(solution)/shard_map/dot_general | solution.py:30
  223.0 0.7 copy-done.6
  223.7 4.9 %psum.7 = f32[1,128]{1,0:T(1,128)S(1)} all-reduce(f32[1,128]{1,0:T(1,128)S(1)} %bitcast.24), channel_id=1, replica_groups=mesh['section'=1,'grp'=16,'tp'=2] {'tp'}, use_global_device_ids=true, to_apply=%region_3.0 | all-reduce | flops 128 | bytes 1024 | tf_op jit(solution)/shard_map/psum | solution.py:16
  228.6 49.7 %reduce-scatter.8.cloned.1.call-done = bf16[1,128,1024]{2,1,0:T(8,128)(2,1)} async-done(((bf16[1,2048,1024]{2,1,0:T(8,128)(2,1)}), bf16[1,128,1024]{2,1,0:T(8,128)(2,1)}) %reduce-scatter.8.cloned.1.call-update) | async-done | bytes 262160 | tf_op jit(solution)/shard_map/reduce_scatter | solution.py:32
  278.3 1.8 add_convert_fusion.2
  280.0 178.9 %reduce-scatter.6.cloned.1.call-done = bf16[1,128,4096]{2,1,0:T(8,128)(2,1)} async-done(((bf16[1,2048,4096]{2,1,0:T(8,128)(2,1)}), bf16[1,128,4096]{2,1,0:T(8,128)(2,1)}) %reduce-scatter.6.cloned.1.call-update) | async-done | bytes 1048592 | tf_op jit(solution)/shard_map/reduce_scatter | solution.py:32
  459.0 2.5 add_convert_fusion
  (21 shorter events, 0.2 us)
Async XLA Ops:
  7.2 194.5 %copy-start = (bf16[512,1024]{1,0:T(8,128)(2,1)S(1)}, bf16[512,1024]{1,0:T(8,128)(2,1)}, u32[]{:S(2)}) copy-start(bf16[512,1024]{1,0:T(8,128)(2,1)} %param.11) | copy-start | bytes 3145732
  7.2 0.8 copy-start.5
  7.2 36.0 %copy-start.3 = (bf16[1,128,4096]{2,1,0:T(8,128)(2,1)S(1)}, bf16[1,128,4096]{2,1,0:T(8,128)(2,1)}, u32[]{:S(2)}) copy-start(bf16[1,128,4096]{2,1,0:T(8,128)(2,1)} %param.8) | copy-start | bytes 3145732
  7.2 35.9 %reduce-scatter.4.cloned.1.call-start = ((), (), s32[]{:S(2)}) async-start(), calls=%async_computation.4 | async-start | bytes 3145728 | tf_op jit(solution)/shard_map/reduce_scatter | solution.py:11
  7.9 72.3 %all-gather.2.cloned.1.call-start = ((), (), s32[]{:S(2)}) async-start(), calls=%async_computation.5 | async-start | bytes 3145728 | tf_op jit(solution)/shard_map/all_gather | solution.py:21
  44.8 1.0 copy-start.1
  47.0 231.3 %reduce-scatter.8.cloned.1.call-start = ((), (), s32[]{:S(2)}) async-start(), calls=%async_computation.7 | async-start | bytes 4456448 | tf_op jit(solution)/shard_map/reduce_scatter | solution.py:32
  207.5 1.6 copy-start.2
  207.5 251.5 %reduce-scatter.6.cloned.1.call-start = ((), (), s32[]{:S(2)}) async-start(), calls=%async_computation.6 | async-start | bytes 17825792 | tf_op jit(solution)/shard_map/reduce_scatter | solution.py:32
  222.9 0.7 copy-start.6
  222.9 0.7 copy-start.4
Sparse Core Ops, SparseCore 0:
  10.2 32.8 reduce-scatter.3
  47.1 33.0 all-gather.1
  207.7 70.5 reduce-scatter.7
  282.2 176.7 reduce-scatter.5

commit v2 on v1

v2 whole, which is shorter than its diff:
```python
import functools
import math

import jax
import jax.numpy as jnp
from jax import lax
from jax.experimental import pallas as pl
from jax.experimental.pallas import tpu as pltpu
from jax.sharding import PartitionSpec as P

epsilon = 1e-06
MESH = pl.DeviceIdType.MESH
CORES = 2
SIDES = 2


def kernel(ranks, width, rows_ref, wq_ref, wk_ref, scale_ref, bias_ref, query_ref, keyval_ref,
           xs, wide, side_out, side_in, rank_out, rank_in, own,
           w_local, w_send, w_recv, x_local, x_send, x_recv, s_send, s_recv, r_send, r_recv):
    me = lax.axis_index("grp")
    core = lax.rem(me, CORES)
    chip = me // CORES
    side = lax.rem(chip, SIDES)
    rank = chip // SIDES
    chips = ranks * SIDES
    mate = chip * CORES + (1 - core)
    depth, q_cols = wq_ref.shape
    k_cols = wk_ref.shape[1]
    share = CORES * depth
    steps = (q_cols + k_cols) // width

    def device(at_rank, at_side):
        return (at_rank * SIDES + at_side) * CORES + core

    barrier = pltpu.get_barrier_semaphore()
    pl.semaphore_signal(barrier, inc=1, device_id={"grp": mate}, device_id_type=MESH)
    for off in range(1, chips):
        to = lax.rem(chip + off, chips) * CORES + core
        pl.semaphore_signal(barrier, inc=1, device_id={"grp": to}, device_id_type=MESH)
    pl.semaphore_wait(barrier, chips)

    def x_copy(off):
        to = lax.rem(chip + off, chips)
        return pltpu.make_async_remote_copy(
            src_ref=rows_ref.at[:, pl.ds(pl.multiple_of(to * share, share), share)],
            dst_ref=xs.at[chip],
            send_sem=x_send.at[off], recv_sem=x_recv.at[chip],
            device_id={"grp": to * CORES + core}, device_id_type=MESH)

    def x_wait(source):
        pltpu.make_async_remote_copy(
            src_ref=rows_ref.at[:, pl.ds(0, share)], dst_ref=xs.at[source],
            send_sem=x_send.at[0], recv_sem=x_recv.at[source],
            device_id={"grp": mate}, device_id_type=MESH).wait_recv()

    x_own = pltpu.make_async_copy(
        rows_ref.at[:, pl.ds(pl.multiple_of(chip * share, share), share)], xs.at[chip], x_local)
    x_own.start()
    offsets = list(range(1, chips))
    for off in offsets:
        x_copy(off).start()

    mine = pl.ds(pl.multiple_of(core * depth, depth), depth)
    q_part = wide.at[mine, pl.ds(0, q_cols)]
    k_part = wide.at[mine, pl.ds(q_cols, k_cols)]
    locals_ = [pltpu.make_async_copy(wq_ref, q_part, w_local.at[0]),
               pltpu.make_async_copy(wk_ref, k_part, w_local.at[1])]
    sends = [pltpu.make_async_remote_copy(
        src_ref=src, dst_ref=dst, send_sem=w_send.at[i], recv_sem=w_recv.at[i],
        device_id={"grp": mate}, device_id_type=MESH)
        for i, (src, dst) in enumerate(((wq_ref, q_part), (wk_ref, k_part)))]
    for copy in sends + locals_:
        copy.start()
    for copy in locals_:
        copy.wait()
    theirs = pl.ds(pl.multiple_of((1 - core) * depth, depth), depth)
    for i, (src, dst) in enumerate(((wq_ref, wide.at[theirs, pl.ds(0, q_cols)]),
                                    (wk_ref, wide.at[theirs, pl.ds(q_cols, k_cols)]))):
        pltpu.make_async_remote_copy(
            src_ref=src, dst_ref=dst, send_sem=w_send.at[i], recv_sem=w_recv.at[i],
            device_id={"grp": mate}, device_id_type=MESH).wait_recv()
    x_own.wait()

    def columns(j):
        return pl.ds(pl.multiple_of(j * width, width), width)

    def s_copy(k, j):
        return pltpu.make_async_remote_copy(
            src_ref=side_out.at[k, :, columns(j)], dst_ref=side_in.at[k, :, columns(j)],
            send_sem=s_send.at[k, j], recv_sem=s_recv.at[k, j],
            device_id={"grp": device(rank, 1 - side)}, device_id_type=MESH)

    def r_copy(k, j):
        return pltpu.make_async_remote_copy(
            src_ref=rank_out.at[k, :, columns(j)], dst_ref=rank_in.at[k, :, columns(j)],
            send_sem=r_send.at[k, j], recv_sem=r_recv.at[k, j],
            device_id={"grp": device(lax.rem(rank + k, ranks), side)}, device_id_type=MESH)

    order = list(range(1, ranks)) + [0]
    for k in order:
        source = lax.rem(rank + k, ranks) * SIDES + (1 - side)
        x_wait(source)

        def body(j, carry, k=k, source=source):
            side_out[k, :, columns(j)] = jnp.dot(
                xs[source], wide[:, columns(j)], preferred_element_type=jnp.float32
            ).astype(jnp.bfloat16)
            s_copy(k, j).start()
            return carry

        lax.fori_loop(0, steps, body, 0)
    for k in order:
        source = lax.rem(rank + k, ranks) * SIDES + side
        if k:
            x_wait(source)

        def body(j, carry, k=k, source=source):
            total = jnp.dot(xs[source], wide[:, columns(j)], preferred_element_type=jnp.float32)
            s_copy(k, j).wait_recv()
            total = total + side_in[k, :, columns(j)].astype(jnp.float32)
            if k:
                rank_out[k, :, columns(j)] = total.astype(jnp.bfloat16)
                r_copy(k, j).start()
            else:
                own[:, columns(j)] = total
            return carry

        lax.fori_loop(0, steps, body, 0)

    def finish(first, count, out_ref):
        def body(i, carry):
            j = first + i
            total = own[:, columns(j)]
            for k in range(1, ranks):
                r_copy(k, j).wait_recv()
                total = total + rank_in[k, :, columns(j)].astype(jnp.float32)
            total = total * scale_ref[...] + bias_ref[:, columns(j)]
            out_ref[:, columns(i)] = total.astype(jnp.bfloat16)
            return carry

        lax.fori_loop(0, count, body, 0)

    finish(0, q_cols // width, query_ref)
    finish(q_cols // width, k_cols // width, keyval_ref)

    for copy in sends:
        copy.wait_send()
    for off in offsets:
        x_copy(off).wait_send()

    def drain(j, carry):
        for k in range(ranks):
            s_copy(k, j).wait_send()
            if k:
                r_copy(k, j).wait_send()
        return carry

    lax.fori_loop(0, steps, drain, 0)


def project(rows, w_query, w_keyval, scale, bias, group):
    count = rows.shape[0]
    depth, q_cols = w_query.shape
    k_cols = w_keyval.shape[1]
    total = q_cols + k_cols
    width = math.gcd(math.gcd(q_cols, k_cols), 512)
    steps = total // width
    ranks = group // (CORES * SIDES)
    chips = group // CORES
    share = CORES * depth
    vmem = pl.BlockSpec(memory_space=pltpu.VMEM)
    hbm = pl.BlockSpec(memory_space=pl.ANY)
    dma = pltpu.SemaphoreType.DMA
    return pl.pallas_call(
        functools.partial(kernel, ranks, width),
        out_shape=(jax.ShapeDtypeStruct((count, q_cols), jnp.bfloat16),
                   jax.ShapeDtypeStruct((count, k_cols), jnp.bfloat16)),
        in_specs=[vmem, hbm, hbm, vmem, vmem],
        out_specs=(vmem, vmem),
        scratch_shapes=[
            pltpu.VMEM((chips, count, share), jnp.bfloat16),
            pltpu.VMEM((share, total), jnp.bfloat16),
            pltpu.VMEM((ranks, count, total), jnp.bfloat16),
            pltpu.VMEM((ranks, count, total), jnp.bfloat16),
            pltpu.VMEM((ranks, count, total), jnp.bfloat16),
            pltpu.VMEM((ranks, count, total), jnp.bfloat16),
            pltpu.VMEM((count, total), jnp.float32),
            dma((2,)), dma((2,)), dma((2,)),
            dma, dma((chips,)), dma((chips,)),
            dma((ranks, steps)), dma((ranks, steps)),
            dma((ranks, steps)), dma((ranks, steps)),
        ],
        compiler_params=pltpu.CompilerParams(
            collective_id=0, has_side_effects=True, vmem_limit_bytes=60 * 1024 * 1024),
    )(rows, w_query, w_keyval, scale, bias)


def local(group, partials, residual, norm_gain, w_query, w_keyval, bias_query, bias_keyval):
    model_width = norm_gain.shape[0]
    summed = lax.psum_scatter(
        partials[0], "tp", scatter_dimension=2, tiled=True
    ).astype(jnp.float32)
    hidden = (residual.astype(jnp.float32) + summed).astype(jnp.bfloat16)
    widened = hidden.astype(jnp.float32)
    squares = lax.psum(jnp.sum(widened * widened, axis=-1), "tp")
    feature_share = widened.shape[2]
    offset = lax.axis_index("tp") * feature_share
    local_gain = lax.dynamic_slice_in_dim(norm_gain, offset, feature_share, 0).astype(jnp.float32)
    scaled = (widened * local_gain).astype(jnp.bfloat16)
    scaled = lax.all_gather(scaled, "tp", axis=2, tiled=True)
    scaled = lax.all_gather(scaled, "section", axis=0, tiled=True)
    squares = lax.all_gather(squares, "section", axis=0, tiled=True)
    seqs, length = squares.shape
    scale = lax.rsqrt(squares / model_width + epsilon).reshape(-1, 1)
    bias = jnp.concatenate([bias_query, bias_keyval]).astype(jnp.float32)[None]
    query, keyval = project(
        scaled.reshape(seqs * length, model_width), w_query, w_keyval, scale, bias, group)
    return (hidden, query.reshape(seqs, length, -1), keyval.reshape(seqs, length, -1))


def solution(mesh):
    placed = (
        P("tp", "section", "grp", None),
        P("section", "grp", "tp"),
        P(),
        P("grp", ("section", "tp")),
        P("grp", ("section", "tp")),
        P(("section", "tp")),
        P(("section", "tp")),
    )
    return jax.shard_map(
        functools.partial(local, mesh.shape["grp"]),
        mesh=mesh,
        in_specs=placed,
        out_specs=(
            P("section", "grp", "tp"),
            P(None, "grp", ("section", "tp")),
            P(None, "grp", ("section", "tp")),
        ),
        check_vma=False,
    )
```

time: 472 us -> 270 us (0.57)
  waiting for transfers between devices: 298 us -> 62.7 us
  Pallas kernels: 0 us -> 181 us
  blocking collectives: 57.2 us -> 4.91 us
  other arithmetic: 52.4 us -> 3.61 us
  local copies, waits for them, and re-layouts: 26.9 us -> 3.83 us
  matrix products: 19.7 us -> 0 us
    reduce_scatter x2 -> x0, waiting for transfers between devices: 229 us -> none  [project(): own = lax.psum_scatter(total, 'grp', scatter_dimension=1, tiled=True)]
    pallas_call x0 -> x1, Pallas kernels: none -> 181 us  [project(): pl.pallas_call(functools.partial(kernel, ranks, width), out_shape=(jax.Sh...]
    all_to_all x1 -> x0, blocking collectives: 52.3 us -> none  [local(): lax.all_to_all(scaled, 'grp', split_axis=2, concat_axis=1, tiled=True)]
    unnamed x1 -> x0, other arithmetic: 45.2 us -> none
    dot_general x2 -> x0, matrix products: 19.7 us -> none  [project(): jnp.dot(flat, weight, preferred_element_type=jnp.float32)]
    unnamed x18 -> x14, local copies, waits for them, and re-layouts: 14.8 us -> 3.06 us
    all_gather x1 -> x0, local copies, waits for them, and re-layouts: 9.49 us -> none  [local(): scaled = lax.all_gather(scaled, 'tp', axis=2, tiled=True)]
    all_gather x1, waiting for transfers between devices: 33.2 us -> 26.9 us  [local(): scaled = lax.all_gather(scaled, 'tp', axis=2, tiled=True)]
  transfers between devices with their start and end apart: 4 -> 2, of which waited for: 4 -> 2; matrix products, arithmetic and copies ran while one was open for 3% -> 1% of each run, Pallas kernels for 0% -> 0%
where the time goes in v2:
time: 270 us
  Pallas kernels  181 us (67%)
  waiting for transfers between devices  62.7 us (23%)
  between operations  14.2 us (5%)
  blocking collectives  4.91 us (2%)
  local copies, waits for them, and re-layouts  3.83 us (1%)
  other arithmetic  3.61 us (1%)
    pallas_call x1, Pallas kernels, project(): pl.pallas_call(functools.partial(kernel, ranks, width), out_shape=(jax.Sh...  181 us
    reduce_scatter x1, waiting for transfers between devices, local(): lax.psum_scatter(partials[0], 'tp', scatter_dimension=2, tiled=True)  35.1 us
    all_gather x1, waiting for transfers between devices, local(): scaled = lax.all_gather(scaled, 'tp', axis=2, tiled=True)  26.9 us
  transfers between devices with their start and end apart: 2, of which 2 were waited for; matrix products, arithmetic and copies ran while one was open for 1% of the time, Pallas kernels for 0%

profile of v2, /device:TPU:26, one launch (start us, length us, event | category | flops | bytes accessed | tf_op | source)
XLA Modules:
  0.0 270.1 jit_solution(6377846510992886149)
XLA Ops:
  7.2 0.0 copy-start.4
  7.2 0.0 copy-start.1
  7.2 0.0 reduce-scatter.2.cloned.1.call-start
  7.2 0.7 reduce-scatter.2.cloned.1.call-update
  7.9 0.0 all-gather.2.cloned.1.call-start
  8.0 0.0 copy-done.4
  8.0 35.1 %reduce-scatter.2.cloned.1.call-done = bf16[1,128,4096]{2,1,0:T(8,128)(2,1)} async-done(((bf16[1,128,8192]{2,1,0:T(8,128)(2,1)}), bf16[1,128,4096]{2,1,0:T(8,128)(2,1)}) %reduce-scatter.2.cloned.1.call-update) | async-done | bytes 1048592 | tf_op jit(solution)/shard_map/reduce_scatter | solution.py:200
  43.1 0.0 copy-done.1
  43.1 1.7 fusion.1
  44.8 0.0 copy-start
  44.8 0.0 copy-start.5
  44.8 0.0 copy-start.3
  44.9 1.3 fusion
  46.1 0.0 all-gather.2.cloned.1.call-update
  46.2 0.0 copy-done.5
  46.2 0.0 copy-done.3
  46.2 0.6 maximum_convert_fusion.bias_ref
  46.8 4.9 %psum.7 = f32[1,128]{1,0:T(1,128)S(1)} all-reduce(f32[1,128]{1,0:T(1,128)S(1)} %bitcast.11), channel_id=1, replica_groups=mesh['section'=1,'grp'=16,'tp'=2] {'tp'}, use_global_device_ids=true, to_apply=%region_2.0 | all-reduce | flops 128 | bytes 1024 | tf_op jit(solution)/shard_map/psum | solution.py:205
  51.8 0.7 copy.10.scale_ref
  52.5 26.9 %all-gather.2.cloned.1.call-done = bf16[1,128,8192]{2,1,0:T(8,128)(2,1)} async-done(((bf16[1,128,4096]{2,1,0:T(8,128)(2,1)}), bf16[1,128,8192]{2,1,0:T(8,128)(2,1)}) %all-gather.2.cloned.1.call-update) | async-done | bytes 2097168 | tf_op jit(solution)/shard_map/all_gather | solution.py:210
  79.4 180.8 %shard_map.94 = (bf16[128,4096]{1,0:T(8,128)(2,1)}, bf16[128,1024]{1,0:T(8,128)(2,1)}) custom-call(bf16[128,8192]{1,0:T(8,128)(2,1)} %bitcast.7, bf16[512,4096]{1,0:T(8,128)(2,1)} %wq_ref.1, bf16[512,1024]{1,0:T(8,128)(2,1)} %wk_ref.1, f32[128,1]{1,0:T(8,128)} %copy.10.scale_ref, f32[1,5120]{1,0:T(1,128)} %maximum_convert_fusion.bias_ref), custom_call_target="tpu_custom_call" | custom-call | tf_op jit(solution)/shard_map/pallas_call | solution.py:174
  260.2 0.0 copy-done
  260.2 2.3 copy.13
  262.5 0.7 copy.14
  (6 shorter events, 0.0 us)
Async XLA Ops:
  7.2 0.8 copy-start.4
  7.2 36.0 %copy-start.1 = (bf16[1,128,4096]{2,1,0:T(8,128)(2,1)S(1)}, bf16[1,128,4096]{2,1,0:T(8,128)(2,1)}, u32[]{:S(2)}) copy-start(bf16[1,128,4096]{2,1,0:T(8,128)(2,1)} %param.8) | copy-start | bytes 3145732
  7.2 35.9 %reduce-scatter.2.cloned.1.call-start = ((), (), s32[]{:S(2)}) async-start(), calls=%async_computation.1 | async-start | bytes 3145728 | tf_op jit(solution)/shard_map/reduce_scatter | solution.py:200
  7.9 71.5 %all-gather.2.cloned.1.call-start = ((), (), s32[]{:S(2)}) async-start(), calls=%async_computation.2 | async-start | bytes 3145728 | tf_op jit(solution)/shard_map/all_gather | solution.py:210
  44.8 215.4 %copy-start = (bf16[1,128,4096]{2,1,0:T(8,128)(2,1)}, bf16[1,128,4096]{2,1,0:T(8,128)(2,1)S(1)}, u32[]{:S(2)}) copy-start(bf16[1,128,4096]{2,1,0:T(8,128)(2,1)S(1)} %get-tuple-element.12) | copy-start | bytes 3145732
  44.8 1.3 copy-start.5
  44.8 1.3 copy-start.3
  260.2 2.3 copy-start.2
Sparse Core Ops, SparseCore 0:
  10.2 32.8 reduce-scatter.1
  46.3 33.0 all-gather.1

commit v3 on v2

--- a/solution.py
+++ b/solution.py
@@ -14,10 +14,12 @@
 SIDES = 2
 
 
-def kernel(ranks, width, rows_ref, wq_ref, wk_ref, scale_ref, bias_ref, query_ref, keyval_ref,
-           xs, wide, side_out, side_in, rank_out, rank_in, own,
-           w_local, w_send, w_recv, x_local, x_send, x_recv, s_send, s_recv, r_send, r_recv):
+def kernel(ranks, parts, width, rows_ref, wq_ref, wk_ref, square_ref, bias_ref,
+           query_ref, keyval_ref, xs, wide, side_out, side_in, rank_out, rank_in, own, squares,
+           w_local, w_send, w_recv, x_local, x_send, x_recv, f_send, f_recv, q_send, q_recv,
+           s_send, s_recv, r_send, r_recv):
     me = lax.axis_index("grp")
+    part = lax.axis_index("tp")
     core = lax.rem(me, CORES)
     chip = me // CORES
     side = lax.rem(chip, SIDES)
@@ -34,31 +36,88 @@
 
     barrier = pltpu.get_barrier_semaphore()
     pl.semaphore_signal(barrier, inc=1, device_id={"grp": mate}, device_id_type=MESH)
-    for off in range(1, chips):
-        to = lax.rem(chip + off, chips) * CORES + core
-        pl.semaphore_signal(barrier, inc=1, device_id={"grp": to}, device_id_type=MESH)
-    pl.semaphore_wait(barrier, chips)
-
-    def x_copy(off):
-        to = lax.rem(chip + off, chips)
-        return pltpu.make_async_remote_copy(
-            src_ref=rows_ref.at[:, pl.ds(pl.multiple_of(to * share, share), share)],
-            dst_ref=xs.at[chip],
-            send_sem=x_send.at[off], recv_sem=x_recv.at[chip],
-            device_id={"grp": to * CORES + core}, device_id_type=MESH)
+    for d in range(parts):
+        for off in range(chips):
+            if d or off:
+                to = lax.rem(chip + off, chips) * CORES + core
+                pl.semaphore_signal(
+                    barrier, inc=1, device_id={"grp": to, "tp": lax.rem(part + d, parts)},
+                    device_id_type=MESH)
+    pl.semaphore_wait(barrier, chips * parts)
+
+    held = chips // parts
+    piece = rows_ref.shape[0] // parts
+    whole_here = chip // held == part
+
+    def piece_of(index):
+        return pl.ds(pl.multiple_of(index * piece, piece), piece)
+
+    def x_ends(i, d):
+        rows = piece_of(lax.rem(part + d, parts))
+        return rows_ref.at[rows, pl.ds(i * share, share)], xs.at[chip, rows]
+
+    def x_copy(i, d):
+        src, dst = x_ends(i, d)
+        return pltpu.make_async_remote_copy(
+            src_ref=src, dst_ref=dst, send_sem=x_send.at[i, d], recv_sem=x_recv.at[chip],
+            device_id={"grp": (part * held + i) * CORES + core, "tp": lax.rem(part + d, parts)},
+            device_id_type=MESH)
+
+    def x_own(i):
+        src, dst = x_ends(i, 0)
+        return pltpu.make_async_copy(src, dst, x_local)
+
+    def each_x(far, near):
+        for i in range(held):
+            here = jnp.logical_and(whole_here, lax.rem(chip, held) == i)
+            pl.when(here)(functools.partial(near, i))
+            pl.when(jnp.logical_not(here))(functools.partial(far, i, 0))
+            for d in range(1, parts):
+                far(i, d)
+
+    each_x(lambda i, d: x_copy(i, d).start(), lambda i: x_own(i).start())
+
+    def q_copy(d):
+        return pltpu.make_async_remote_copy(
+            src_ref=square_ref, dst_ref=squares.at[d],
+            send_sem=q_send.at[d], recv_sem=q_recv.at[d],
+            device_id={"tp": lax.rem(part + d, parts)}, device_id_type=MESH)
+
+    for d in range(1, parts):
+        q_copy(d).start()
+
+    def x_arrive(source):
+        pltpu.make_async_remote_copy(
+            src_ref=xs.at[source, piece_of(part)], dst_ref=xs.at[source, piece_of(part)],
+            send_sem=x_send.at[0, 0], recv_sem=x_recv.at[source],
+            device_id={"grp": mate}, device_id_type=MESH).wait_recv()
+
+    def f_copy(source, d):
+        return pltpu.make_async_remote_copy(
+            src_ref=xs.at[source, piece_of(part)], dst_ref=xs.at[source, piece_of(part)],
+            send_sem=f_send.at[source, d], recv_sem=f_recv.at[source, d],
+            device_id={"tp": lax.rem(part + d, parts)}, device_id_type=MESH)
+
+    def pass_on(source, here):
+        if here:
+            def near():
+                for i in range(held):
+                    pl.when(lax.rem(chip, held) == i)(lambda i=i: x_own(i).wait())
+
+            pl.when(whole_here)(near)
+            pl.when(jnp.logical_not(whole_here))(lambda: x_arrive(source))
+        else:
+            x_arrive(source)
+        for d in range(1, parts):
+            f_copy(source, d).start()
 
     def x_wait(source):
-        pltpu.make_async_remote_copy(
-            src_ref=rows_ref.at[:, pl.ds(0, share)], dst_ref=xs.at[source],
-            send_sem=x_send.at[0], recv_sem=x_recv.at[source],
-            device_id={"grp": mate}, device_id_type=MESH).wait_recv()
-
-    x_own = pltpu.make_async_copy(
-        rows_ref.at[:, pl.ds(pl.multiple_of(chip * share, share), share)], xs.at[chip], x_local)
-    x_own.start()
-    offsets = list(range(1, chips))
-    for off in offsets:
-        x_copy(off).start()
+        for d in range(1, parts):
+            rows = piece_of(lax.rem(part + parts - d, parts))
+            pltpu.make_async_remote_copy(
+                src_ref=xs.at[source, rows], dst_ref=xs.at[source, rows],
+                send_sem=f_send.at[source, d], recv_sem=f_recv.at[source, d],
+                device_id={"grp": mate}, device_id_type=MESH).wait_recv()
 
     mine = pl.ds(pl.multiple_of(core * depth, depth), depth)
     q_part = wide.at[mine, pl.ds(0, q_cols)]
@@ -79,7 +138,6 @@
         pltpu.make_async_remote_copy(
             src_ref=src, dst_ref=dst, send_sem=w_send.at[i], recv_sem=w_recv.at[i],
             device_id={"grp": mate}, device_id_type=MESH).wait_recv()
-    x_own.wait()
 
     def columns(j):
         return pl.ds(pl.multiple_of(j * width, width), width)
@@ -99,6 +157,8 @@
     order = list(range(1, ranks)) + [0]
     for k in order:
         source = lax.rem(rank + k, ranks) * SIDES + (1 - side)
+        pass_on(source, False)
+        pass_on(lax.rem(rank + k, ranks) * SIDES + side, k == 0)
         x_wait(source)
 
         def body(j, carry, k=k, source=source):
@@ -111,8 +171,7 @@
         lax.fori_loop(0, steps, body, 0)
     for k in order:
         source = lax.rem(rank + k, ranks) * SIDES + side
-        if k:
-            x_wait(source)
+        x_wait(source)
 
         def body(j, carry, k=k, source=source):
             total = jnp.dot(xs[source], wide[:, columns(j)], preferred_element_type=jnp.float32)
@@ -127,6 +186,13 @@
 
         lax.fori_loop(0, steps, body, 0)
 
+    mean_square = square_ref[...]
+    for d in range(1, parts):
+        q_copy(d).wait_recv()
+        mean_square = mean_square + squares[d]
+    model_width = rows_ref.shape[1] * parts
+    scale = lax.rsqrt(mean_square[:, :1] / model_width + epsilon)
+
     def finish(first, count, out_ref):
         def body(i, carry):
             j = first + i
@@ -134,7 +200,7 @@
             for k in range(1, ranks):
                 r_copy(k, j).wait_recv()
                 total = total + rank_in[k, :, columns(j)].astype(jnp.float32)
-            total = total * scale_ref[...] + bias_ref[:, columns(j)]
+            total = total * scale + bias_ref[:, columns(j)]
             out_ref[:, columns(i)] = total.astype(jnp.bfloat16)
             return carry
 
@@ -145,8 +211,11 @@
 
     for copy in sends:
         copy.wait_send()
-    for off in offsets:
-        x_copy(off).wait_send()
+    each_x(lambda i, d: x_copy(i, d).wait_send(), lambda i: None)
+    for d in range(1, parts):
+        q_copy(d).wait_send()
+        for source in range(chips):
+            f_copy(source, d).wait_send()
 
     def drain(j, carry):
         for k in range(ranks):
@@ -158,7 +227,7 @@
     lax.fori_loop(0, steps, drain, 0)
 
 
-def project(rows, w_query, w_keyval, scale, bias, group):
+def project(rows, w_query, w_keyval, squares, bias, group, parts):
     count = rows.shape[0]
     depth, q_cols = w_query.shape
     k_cols = w_keyval.shape[1]
@@ -172,7 +241,7 @@
     hbm = pl.BlockSpec(memory_space=pl.ANY)
     dma = pltpu.SemaphoreType.DMA
     return pl.pallas_call(
-        functools.partial(kernel, ranks, width),
+        functools.partial(kernel, ranks, parts, width),
         out_shape=(jax.ShapeDtypeStruct((count, q_cols), jnp.bfloat16),
                    jax.ShapeDtypeStruct((count, k_cols), jnp.bfloat16)),
         in_specs=[vmem, hbm, hbm, vmem, vmem],
@@ -185,36 +254,46 @@
             pltpu.VMEM((ranks, count, total), jnp.bfloat16),
             pltpu.VMEM((ranks, count, total), jnp.bfloat16),
             pltpu.VMEM((count, total), jnp.float32),
+            pltpu.VMEM((parts, count, squares.shape[1]), jnp.float32),
             dma((2,)), dma((2,)), dma((2,)),
-            dma, dma((chips,)), dma((chips,)),
+            dma, dma((chips // parts, parts)), dma((chips,)),
+            dma((chips, parts)), dma((chips, parts)), dma((parts,)), dma((parts,)),
             dma((ranks, steps)), dma((ranks, steps)),
             dma((ranks, steps)), dma((ranks, steps)),
         ],
         compiler_params=pltpu.CompilerParams(
             collective_id=0, has_side_effects=True, vmem_limit_bytes=60 * 1024 * 1024),
-    )(rows, w_query, w_keyval, scale, bias)
-
-
-def local(group, partials, residual, norm_gain, w_query, w_keyval, bias_query, bias_keyval):
-    model_width = norm_gain.shape[0]
-    summed = lax.psum_scatter(
-        partials[0], "tp", scatter_dimension=2, tiled=True
-    ).astype(jnp.float32)
+    )(rows, w_query, w_keyval, squares, bias)
+
+
+def own_sum(partial, feature_share, parts):
+    if parts != 2:
+        return lax.psum_scatter(
+            partial, "tp", scatter_dimension=2, tiled=True).astype(jnp.float32)
+    part = lax.axis_index("tp")
+    own = lax.dynamic_slice_in_dim(partial, part * feature_share, feature_share, 2)
+    other = lax.dynamic_slice_in_dim(partial, (1 - part) * feature_share, feature_share, 2)
+    other = lax.ppermute(other, "tp", [(0, 1), (1, 0)])
+    return own.astype(jnp.float32) + other.astype(jnp.float32)
+
+
+def local(group, parts, partials, residual, norm_gain, w_query, w_keyval, bias_query, bias_keyval):
+    feature_share = residual.shape[2]
+    summed = own_sum(partials[0], feature_share, parts)
     hidden = (residual.astype(jnp.float32) + summed).astype(jnp.bfloat16)
     widened = hidden.astype(jnp.float32)
-    squares = lax.psum(jnp.sum(widened * widened, axis=-1), "tp")
-    feature_share = widened.shape[2]
+    squares = jnp.sum(widened * widened, axis=-1)
     offset = lax.axis_index("tp") * feature_share
     local_gain = lax.dynamic_slice_in_dim(norm_gain, offset, feature_share, 0).astype(jnp.float32)
     scaled = (widened * local_gain).astype(jnp.bfloat16)
-    scaled = lax.all_gather(scaled, "tp", axis=2, tiled=True)
     scaled = lax.all_gather(scaled, "section", axis=0, tiled=True)
     squares = lax.all_gather(squares, "section", axis=0, tiled=True)
     seqs, length = squares.shape
-    scale = lax.rsqrt(squares / model_width + epsilon).reshape(-1, 1)
+    squares = jnp.broadcast_to(squares.reshape(-1, 1), (seqs * length, 128))
     bias = jnp.concatenate([bias_query, bias_keyval]).astype(jnp.float32)[None]
     query, keyval = project(
-        scaled.reshape(seqs * length, model_width), w_query, w_keyval, scale, bias, group)
+        scaled.reshape(seqs * length, feature_share), w_query, w_keyval, squares, bias,
+        group, parts)
     return (hidden, query.reshape(seqs, length, -1), keyval.reshape(seqs, length, -1))
 
 
@@ -229,7 +308,7 @@
         P(("section", "tp")),
     )
     return jax.shard_map(
-        functools.partial(local, mesh.shape["grp"]),
+        functools.partial(local, mesh.shape["grp"], mesh.shape["tp"]),
         mesh=mesh,
         in_specs=placed,
         out_specs=(

time: 270 us -> 233 us (0.86)
  waiting for transfers between devices: 62.7 us -> 22.8 us
  Pallas kernels: 181 us -> 198 us
  between operations: 14.2 us -> 0.74 us
  blocking collectives: 4.91 us -> 0 us
    reduce_scatter x1 -> x0, waiting for transfers between devices: 35.1 us -> none  [local(): lax.psum_scatter(partials[0], 'tp', scatter_dimension=2, tiled=True)]
    all_gather x1 -> x0, waiting for transfers between devices: 26.9 us -> none  [local(): scaled = lax.all_gather(scaled, 'tp', axis=2, tiled=True)]
    ppermute x0 -> x1, waiting for transfers between devices: none -> 22.8 us  [own_sum(): other = lax.ppermute(other, 'tp', [(0, 1), (1, 0)])]
    pallas_call x1, Pallas kernels: 181 us -> 198 us  [project(): pl.pallas_call(functools.partial(kernel, ranks, parts, width), out_shape=...]
    psum x1 -> x0, blocking collectives: 4.91 us -> none  [local(): squares = lax.psum(jnp.sum(widened * widened, axis=-1), 'tp')]
  transfers between devices with their start and end apart: 2 -> 1, of which waited for: 2 -> 1; matrix products, arithmetic and copies ran while one was open for 1% -> 0% of each run, Pallas kernels for 0% -> 0%
where the time goes in v3:
time: 233 us
  Pallas kernels  198 us (85%)
  waiting for transfers between devices  22.8 us (10%)
  local copies, waits for them, and re-layouts  5.23 us (2%)
  other arithmetic  4.08 us (2%)
    pallas_call x1, Pallas kernels, project(): pl.pallas_call(functools.partial(kernel, ranks, parts, width), out_shape=...  198 us
    ppermute x1, waiting for transfers between devices, own_sum(): other = lax.ppermute(other, 'tp', [(0, 1), (1, 0)])  22.8 us
  transfers between devices with their start and end apart: 1, of which 1 were waited for; matrix products, arithmetic and copies ran while one was open for 0% of the time, Pallas kernels for 0%

profile of v3, /device:TPU:26, one launch (start us, length us, event | category | flops | bytes accessed | tf_op | source)
XLA Modules:
  0.0 232.8 jit_solution(2916359718282102550)
XLA Ops:
  0.6 0.0 copy-start.1
  0.6 0.0 copy-start.5
  0.7 0.0 copy-start.3
  0.7 0.0 copy-start.4
  0.7 1.4 dynamic-slice_bitcast_fusion
  2.1 1.6 collective-permute-start
  3.7 0.0 copy-done.5
  3.7 0.0 copy-done.3
  3.7 0.0 copy-done.4
  3.8 0.6 maximum_convert_fusion.bias_ref
  4.4 22.8 %collective-permute-done = bf16[1,128,4096]{2,1,0:T(8,128)(2,1)} collective-permute-done((bf16[1,128,4096]{2,1,0:T(8,128)(2,1)S(1)}, bf16[1,128,4096]{2,1,0:T(8,128)(2,1)}, u32[]{:S(2)}, u32[]{:S(2)}) %collective-permute-start) | collective-permute-done | bytes 1048608 | tf_op jit(solution)/shard_map/ppermute | solution.py:276
  27.2 0.0 copy-done.1
  27.2 2.1 fusion.1
  29.3 0.0 copy-start
  29.3 1.3 fusion.4.rows_ref
  30.6 0.7 broadcast_in_dim.2.square_ref
  31.4 198.4 %shard_map.94 = (bf16[128,4096]{1,0:T(8,128)(2,1)}, bf16[128,1024]{1,0:T(8,128)(2,1)}) custom-call(bf16[128,4096]{1,0:T(8,128)(2,1)} %fusion.4.rows_ref, bf16[512,4096]{1,0:T(8,128)(2,1)} %wq_ref.1, bf16[512,1024]{1,0:T(8,128)(2,1)} %wk_ref.1, f32[128,128]{1,0:T(8,128)} %broadcast_in_dim.2.square_ref, f32[1,5120]{1,0:T(1,128)} %maximum_convert_fusion.bias_ref), custom_call_target="tpu_custom_call" | custom-call | tf_op jit(solution)/shard_map/pallas_call | solution.py:243
  229.8 0.0 copy-done
  229.8 0.0 copy-start.2
  229.8 2.3 %copy.12 = bf16[1,128,4096]{2,1,0:T(8,128)(2,1)} copy(bf16[1,128,4096]{2,1,0:T(8,128)(2,1)} %bitcast.10) | data formatting | bytes 2097152
  232.1 0.0 copy-done.2
  232.1 0.7 copy.13
  (3 shorter events, 0.0 us)
Async XLA Ops:
  0.6 26.6 %copy-start.1 = (bf16[1,1,128,8192]{3,2,1,0:T(8,128)(2,1)S(1)}, bf16[1,1,128,8192]{3,2,1,0:T(8,128)(2,1)}, u32[]{:S(2)}) copy-start(bf16[1,1,128,8192]{3,2,1,0:T(8,128)(2,1)} %param.7) | copy-start | bytes 6291460
  0.6 3.1 %copy-start.5 = (bf16[1024]{0:T(1024)(128)(2,1)S(1)}, bf16[1024]{0:T(1024)(128)(2,1)}, u32[]{:S(2)}) copy-start(bf16[1024]{0:T(1024)(128)(2,1)} %param.13) | copy-start | bytes 6148
  0.7 3.1 %copy-start.3 = (bf16[4096]{0:T(1024)(128)(2,1)S(1)}, bf16[4096]{0:T(1024)(128)(2,1)}, u32[]{:S(2)}) copy-start(bf16[4096]{0:T(1024)(128)(2,1)} %param.12) | copy-start | bytes 24580
  0.7 3.1 %copy-start.4 = (bf16[8192]{0:T(1024)(128)(2,1)S(1)}, bf16[8192]{0:T(1024)(128)(2,1)}, u32[]{:S(2)}) copy-start(bf16[8192]{0:T(1024)(128)(2,1)} %param.9) | copy-start | bytes 49156
  2.1 25.1 %collective-permute-start = (bf16[1,128,4096]{2,1,0:T(8,128)(2,1)S(1)}, bf16[1,128,4096]{2,1,0:T(8,128)(2,1)}, u32[]{:S(2)}, u32[]{:S(2)}) collective-permute-start(bf16[1,128,4096]{2,1,0:T(8,128)(2,1)S(1)} %dynamic-slice_bitcast_fusion), channel_id=1, source_target_pairs={{0,1},{1,0},{2,3},{3,2},{4,5},{5,4},{6,7},{7,6},{8,9},{9,8},{10,11... | collective-permute-start | bytes 3145736 | tf_op jit(solution)/shard_map/ppermute | solution.py:276
  29.3 200.4 %copy-start = (bf16[1,128,4096]{2,1,0:T(8,128)(2,1)}, bf16[1,128,4096]{2,1,0:T(8,128)(2,1)S(1)}, u32[]{:S(2)}) copy-start(bf16[1,128,4096]{2,1,0:T(8,128)(2,1)S(1)} %get-tuple-element.12) | copy-start | bytes 3145732
  229.8 2.3 %copy-start.2 = (bf16[128,1024]{1,0:T(8,128)(2,1)S(1)}, bf16[128,1024]{1,0:T(8,128)(2,1)}, u32[]{:S(2)}) copy-start(bf16[128,1024]{1,0:T(8,128)(2,1)} %get-tuple-element.6) | copy-start | bytes 786436
